TPU v7x, 128 devices: a whole 4x4x4 slice. The times are simulated.
128 devices in a mesh: fit: 8 (over z, core), pair: 16 (over x, y).
Axes of the slice: x: 4, y: 4, z: 4, core: 2. Of those that a mesh axis runs over, the one named last changes fastest.
Arguments:
- metric_factor: bfloat16 [4096, 4096], P('fit'), as said below
- three_index: bfloat16 [4096, 32768], P('fit', 'pair'), may hold values from -6 to 6
- send_map: int32 [16, 16, 8], P('pair'), may hold values from 0 to 15
- pair_slots: int32 [16, 128], P('pair'), may hold values from 0 to 127, each once within a row
- pair_count: int32 [16], P('pair'), may hold values from 1 to 64, 512 in all
- orbital_energy: bfloat16 [256], P('pair'), may hold values from -2 to -0.19921875
- cabs_energy: float32 [1024], replicated, may hold values from 0.5 to 4
- coupling: bfloat16 [128, 1024], replicated, may hold values from -0.5 to 0.5
Outputs:
- projected: bfloat16 [16, 64, 128, 1024], P('pair', 'fit')
Inputs may be any that keep to these rules, and one draw needn't show every extreme that they name: `metric_factor`: diagonal entries lie between 0.6 and 1.4. `pair_slots`: each row holds every position 0 to 127 once; pair n of a row uses entries 2n and 2n + 1.
All inputs are finite; a program needn't handle non-finite values. No bound on the sum of `pair_count` on one device may be relied on, other than what follows from the above.
Results may differ from a plain program's by a relative error of at most 0.015.
Values may be sent and summed in bfloat16 or wider, within the bound.
A program may use at most 256 MiB of HBM per device.

v0:
```python
import jax
import jax.numpy as jnp
from jax import lax
from jax.sharding import PartitionSpec as P

NAUX = 4096
PAIR_BLOCK = 8


def turned_gather(arrays, axis, dims):
    turned = [jnp.moveaxis(a, dim, 0) for a, dim in zip(arrays, dims)]
    both = jnp.concatenate([t.reshape(len(t), -1) for t in turned], axis=1)
    filled, at, outs = (lax.all_gather(both, axis, axis=0, tiled=True), 0, [])
    for t, dim in zip(turned, dims):
        slab = filled[:, at : at + t[0].size].reshape(-1, *t.shape[1:])
        outs.append(jnp.moveaxis(slab, 0, dim))
        at += t[0].size
    return tuple(outs)


def on_device(
    metric_factor,
    three_index,
    send_map,
    pair_slots,
    pair_count,
    orbital_energy,
    cabs_energy,
    coupling,
):
    domain = coupling.shape[0]
    orbitals = orbital_energy.shape[0]
    local_rows = metric_factor.shape[0]
    peers = send_map.shape[1]
    capacity = send_map.shape[2]
    slot_total = pair_slots.shape[1] // 2
    fitted = jnp.dot(
        metric_factor,
        lax.all_gather(three_index, "fit", axis=0, tiled=True),
        preferred_element_type=jnp.float32,
    )
    fitted = fitted.astype(jnp.bfloat16).reshape(local_rows, orbitals, domain)
    requests = send_map.reshape(peers, capacity)
    source, energy_src = turned_gather((fitted, orbital_energy), "pair", (1, 0))
    global_ids = (jnp.arange(peers, dtype=jnp.int32)[:, None] * orbitals + requests).reshape(-1)
    pair_index = jnp.take(global_ids, pair_slots[0])
    left_index = pair_index[0::2]
    right_index = pair_index[1::2]
    live_count = pair_count[0]
    norm_scale = NAUX ** (-0.5)
    block_count = (live_count + PAIR_BLOCK - 1) // PAIR_BLOCK

    def advance(block, partial_value):
        left_ids = lax.dynamic_slice_in_dim(left_index, block * PAIR_BLOCK, PAIR_BLOCK)
        right_ids = lax.dynamic_slice_in_dim(right_index, block * PAIR_BLOCK, PAIR_BLOCK)
        left_rows = jnp.take(source, left_ids, axis=1)
        right_rows = jnp.take(source, right_ids, axis=1)
        product = jnp.einsum(
            "qsa,qsb->sab", left_rows, right_rows, preferred_element_type=jnp.float32
        )
        return lax.dynamic_update_slice_in_dim(
            partial_value, product * norm_scale, block * PAIR_BLOCK, 0
        )

    partial_value = jnp.zeros((slot_total, domain, domain), jnp.float32)
    partial_value = lax.fori_loop(0, block_count, advance, partial_value)
    share = slot_total // lax.axis_size("fit")
    first_slot = lax.axis_index("fit") * share
    exchange = lax.psum_scatter(
        partial_value.astype(jnp.bfloat16), "fit", scatter_dimension=0, tiled=True
    )
    energy_sum = jnp.take(energy_src, left_index).astype(jnp.float32) + jnp.take(
        energy_src, right_index
    ).astype(jnp.float32)
    energy_sum = lax.dynamic_slice_in_dim(energy_sum, first_slot, share, 0)
    weighted = jnp.einsum("sab,bc->sac", exchange, coupling, preferred_element_type=jnp.float32)
    denom = cabs_energy[None, None, :] - energy_sum[:, None, None]
    live_mask = first_slot + jnp.arange(share, dtype=jnp.int32) < live_count
    projected = jnp.where(live_mask[:, None, None], weighted / denom, 0.0).astype(jnp.bfloat16)
    return projected.reshape(1, share, domain, weighted.shape[2])


def solution(mesh):
    in_specs = (
        P("fit", None),
        P("fit", "pair"),
        P("pair", None, None),
        P("pair", None),
        P("pair"),
        P("pair"),
        P(),
        P(),
    )
    out_specs = P("pair", "fit", None, None)
    return jax.shard_map(
        on_device, mesh=mesh, in_specs=in_specs, out_specs=out_specs, check_vma=False
    )
```

profile of v0, /device:TPU:1, one launch (start us, length us, event | category | flops | bytes accessed | tf_op | source)
XLA Modules:
  0.0 505.2 jit_solution(18273993454955358155)
XLA Ops:
  6.5 0.0 copy-start
  6.5 0.0 all-gather.3.cloned.1.call-start
  6.5 0.7 all-gather.3.cloned.1.call-update
  7.3 0.0 all-gather.5.cloned.1.call-start
  7.3 0.7 copy.16
  8.1 89.8 %all-gather.3.cloned.1.call-done = bf16[4096,2048]{1,0:T(8,128)(2,1)} async-done(((bf16[512,2048]{1,0:T(8,128)(2,1)}), bf16[4096,2048]{1,0:T(8,128)(2,1)}) %all-gather.3.cloned.1.call-update) | async-done | bytes 16777232 | tf_op jit(solution)/shard_map/all_gather | solution.py:39
  97.8 13.6 %fusion.9 = bf16[64,16,8,128]{3,2,1,0:T(8,128)(2,1)S(1)} fusion(bf16[512,4096]{1,0:T(8,128)(2,1)} %param.14, bf16[4096,2048]{1,0:T(8,128)(2,1)} %all-gather.3.cloned.1.call-done), kind=kOutput, calls=%fused_computation.26 | convolution fusion | flops 8590983168 | bytes 23068672 | tf_op jit(solution)/shard_map/dot_general | solution.py:37
  111.4 0.5 copy.25
  112.0 1.4 copy.24
  113.3 0.0 copy-start.1
  113.3 0.0 copy-start.3
  113.3 1.5 pad_maximum_fusion
  114.8 0.0 all-gather.5.cloned.1.call-update
  114.8 0.0 reduce-scatter.2.cloned.1.call-start
  115.5 0.1 add.76
  115.6 0.1 add.77
  115.7 0.0 copy-done.1
  115.7 0.1 copy.14
  115.8 0.1 reshape.106
  115.9 0.0 copy-done.3
  115.9 1.2 gather_fusion.2
  117.2 0.2 slice.14
  117.3 0.2 slice.12
  117.5 194.5 %all-gather.5.cloned.1.call-done = bf16[256,65537]{1,0:T(8,128)(2,1)} async-done(((bf16[16,65537]{1,0:T(8,128)(2,1)}), bf16[256,65537]{1,0:T(8,128)(2,1)}) %all-gather.5.cloned.1.call-update) | async-done | bytes 33554960 | tf_op jit(solution)/shard_map/all_gather | solution.py:13
  312.0 22.9 %slice.26 = bf16[256,65536]{1,0:T(8,128)(2,1)} slice(bf16[256,65537]{1,0:T(8,128)(2,1)} %all-gather.5.cloned.1.call-done), slice={[0:256], [0:65536]} | slice | bytes 67108864 | tf_op jit(solution)/shard_map/slice | solution.py:15
  334.9 41.6 %copy.17 = bf16[256,65536]{0,1:T(8,128)(2,1)} copy(bf16[256,65536]{1,0:T(8,128)(2,1)} %slice.26) | data formatting | bytes 67108864 | tf_op jit(solution)/shard_map/slice | solution.py:15
  376.4 43.8 %copy.18 = bf16[512,256,128]{2,0,1:T(8,128)(2,1)} copy(bf16[512,256,128]{1,2,0:T(8,128)(2,1)} %bitcast.41) | data formatting | bytes 67108864 | tf_op jit(solution)/shard_map/while | solution.py:66
  420.2 1.8 broadcast_in_dim.41
  422.0 0.0 copy-start.2
  422.0 21.3 %while.10 = (s32[]{:T(128)}, bf16[64,128,128]{2,1,0:T(8,128)(2,1)}, s32[]{:T(128)}, s32[64]{0:T(128)S(1)}, bf16[512,256,128]{2,0,1:T(8,128)(2,1)}, /*index=5*/s3...) while((s32[]{:T(128)}, bf16[64,128,128]{2,1,0:T(8,128)(2,1)}, s32[]{:T(128)}, s32[64]{0:T(128)S(1)}, ...), condition=%wide.region_1.3_spmd, body=%wide.region_0.0_spmd.sunk | while | flops 135399520 | bytes 6824379 | solution.py:66
  422.0 0.1 compare_and_fusion.3
  422.1 2.0 gather_fusion.1
  424.1 2.0 gather_fusion
  426.1 1.3 fusion.21
  427.4 0.1 compare_and_fusion.3
  427.5 2.0 gather_fusion.1
  429.4 2.0 gather_fusion
  431.4 1.3 fusion.21
  432.7 0.1 compare_and_fusion.3
  432.8 2.0 gather_fusion.1
  434.8 2.0 gather_fusion
  436.7 1.3 fusion.21
  438.0 0.1 compare_and_fusion.3
  438.1 2.0 gather_fusion.1
  440.1 2.0 gather_fusion
  442.0 1.3 fusion.21
  443.3 0.0 reduce-scatter.2.cloned.1.call-update
  443.4 0.9 slice_reduce_fusion
  444.4 0.8 gather_fusion.4
  445.2 0.8 gather_fusion.3
  446.0 0.1 dynamic_slice.9
  446.0 0.0 copy-done.2
  446.0 0.1 broadcast_subtract_fusion
  446.1 49.6 %reduce-scatter.2.cloned.1.call-done = bf16[8,128,128]{2,1,0:T(8,128)(2,1)} async-done(((bf16[64,128,128]{2,1,0:T(8,128)(2,1)}), bf16[8,128,128]{2,1,0:T(8,128)(2,1)}) %reduce-scatter.2.cloned.1.call-update) | async-done | bytes 262160 | tf_op jit(solution)/shard_map/reduce_scatter | solution.py:69
  495.7 0.0 copy-done
  495.8 3.0 fusion.10
  (19 shorter events, 0.1 us)
Async XLA Ops:
  6.5 489.2 %copy-start = (bf16[128,1024]{1,0:T(8,128)(2,1)S(1)}, bf16[128,1024]{1,0:T(8,128)(2,1)}, u32[]{:S(2)}) copy-start(bf16[128,1024]{1,0:T(8,128)(2,1)} %param.21) | copy-start | bytes 786436
  6.5 91.3 %all-gather.3.cloned.1.call-start = ((), (), s32[]{:S(2)}) async-start(), calls=%async_computation.1 | async-start | bytes 18874368 | tf_op jit(solution)/shard_map/all_gather | solution.py:39
  7.3 304.8 %all-gather.5.cloned.1.call-start = ((), (), s32[]{:S(2)}) async-start(), calls=%async_computation.2 | async-start | bytes 35721216 | tf_op jit(solution)/shard_map/all_gather | solution.py:13
  113.3 2.4 copy-start.1
  113.3 2.6 copy-start.3
  114.8 380.9 %reduce-scatter.2.cloned.1.call-start = ((), (), s32[]{:S(2)}) async-start(), calls=%async_computation.3 | async-start | bytes 2359296 | tf_op jit(solution)/shard_map/reduce_scatter | solution.py:69
  422.0 24.0 %copy-start.2 = (f32[1024]{0:T(1024)S(1)}, f32[1024]{0:T(1024)}, u32[]{:S(2)}) copy-start(f32[1024]{0:T(1024)} %param.20) | copy-start | bytes 12292
Sparse Core Ops, SparseCore 0:
  9.0 88.7 all-gather.2
  114.9 197.0 all-gather.4
  443.5 52.2 reduce-scatter.1
where the time goes:
time: 510 us; the launch traced here: 505 us
  waiting for transfers between devices  335 us (66%)
  local copies, waits for them, and re-layouts  133 us (26%)
  matrix products  21.7 us (4%)
  between operations  13.9 us (3%)
    all_gather x1, waiting for transfers between devices, turned_gather(): filled, at, outs = (lax.all_gather(both, axis, axis=0, tiled=True), 0, [])  195 us
    all_gather x1, waiting for transfers between devices, on_device(): lax.all_gather(three_index, 'fit', axis=0, tiled=True)  89.8 us
    slice x3, local copies, waits for them, and re-layouts, turned_gather(): slab = filled[:, at:at + t[0].size].reshape(-1, *t.shape[1:])  65.4 us
    reduce_scatter x1, waiting for transfers between devices, on_device(): lax.psum_scatter(partial_value.astype(jnp.bfloat16), 'fit', scatter_dimen...  49.6 us
    while x1, local copies, waits for them, and re-layouts, on_device(): partial_value = lax.fori_loop(0, block_count, advance, partial_value)  43.8 us
    dot_general x1, matrix products, on_device(): jnp.dot(metric_factor, lax.all_gather(three_index, 'fit', axis=0, tiled=T...  13.6 us
  transfers between devices with their start and end apart: 3, of which 3 were waited for; matrix products, arithmetic and copies ran while one was open for 1% of the time, Pallas kernels for 0%

commit v1 on v0

v1 whole, which is shorter than its diff:
```python
import jax
import jax.numpy as jnp
from jax import lax
from jax.experimental import pallas as pl
from jax.experimental.pallas import tpu as pltpu
from jax.sharding import PartitionSpec as P

MESH = pl.DeviceIdType.MESH
F32 = jnp.float32
BF16 = jnp.bfloat16
CHUNKS = 8
LANES = 128
PANEL = 512
QROWS = 256
SCALE = 4096.0 ** -0.5


def fused_kernel(
    fac, tri, ints, ens, cabs,
    exch_out, rec_out,
    a_v, b_v, f_v, cols, part, rs1, summed, rs2, ints_v, ens_v, ints_s, ens_s,
    a_sem, zs, zr, xs, xr, ys, yr, ps, pr, i_sem, e_sem, r_sem, l_sem,
):
    f = lax.axis_index("fit")
    p = lax.axis_index("pair")
    z, c = f // 2, f % 2
    x, y = p // 4, p % 4
    nc = 1 - c
    zp, zm, zo = (z + 1) % 4, (z + 3) % 4, (z + 2) % 4
    yp, ym, yo = (y + 1) % 4, (y + 3) % 4, (y + 2) % 4

    def dev(zz, cc, xx, yy):
        return (2 * zz + cc, 4 * xx + yy)

    me_partner = dev(z, nc, x, y)

    def remote(src, dst, ss, rs, to):
        return pltpu.make_async_remote_copy(
            src_ref=src, dst_ref=dst, send_sem=ss, recv_sem=rs, device_id=to, device_id_type=MESH
        )

    barrier = pltpu.get_barrier_semaphore()
    greeted = [me_partner]
    for d in (1, 2, 3):
        greeted.append(dev((z + d) % 4, c, x, y))
        greeted.append(dev(z, c, (x + d) % 4, y))
        greeted.append(dev(z, c, x, (y + d) % 4))
    greeted.append(dev(zp, nc, x, y))
    greeted.append(dev(zm, nc, x, y))
    for to in greeted:
        pl.semaphore_signal(barrier, inc=1, device_id=to, device_id_type=MESH)
    pl.semaphore_wait(barrier, len(greeted))

    def own_src(h, g):
        return tri.at[:, pl.ds(pl.multiple_of((h * CHUNKS + g) * LANES, LANES), LANES)]

    def panel(g, k):
        return b_v.at[g, pl.ds(pl.multiple_of(k * PANEL, PANEL), PANEL), :]

    def own_copies(g):
        out = []
        for i, (zz, h) in enumerate(((zp, 0), (zm, 0), (zp, 1), (zm, 1))):
            out.append(remote(own_src(h, g), panel(g, f), zs.at[g, i], zr.at[g, f], dev(zz, h, x, y)))
        out.append(remote(own_src(nc, g), panel(g, f), zs.at[g, 4], zr.at[g, f], me_partner))
        return out

    def own_local(g):
        return pltpu.make_async_copy(own_src(c, g), panel(g, f), l_sem.at[g])

    def z_wait(g, k):
        remote(panel(g, k), panel(g, k), zs.at[g, 0], zr.at[g, k], me_partner).wait_recv()

    def z_forwards(g):
        return (
            remote(panel(g, 2 * zm), panel(g, 2 * zm), zs.at[g, 5], zr.at[g, 2 * zm], dev(zp, c, x, y)),
            remote(panel(g, 2 * zp + 1), panel(g, 2 * zp + 1), zs.at[g, 6], zr.at[g, 2 * zp + 1], dev(zm, c, x, y)),
        )

    def col_at(cc, yy, g):
        return ((cc * 4 + yy) * CHUNKS + g) * 4

    def x_copies(g):
        out = []
        for i, d in enumerate((2, 1, 3)):
            to = (x + d) % 4
            out.append(remote(f_v.at[g, to], cols.at[col_at(c, y, g) + x], xs.at[g, i], xr.at[g, i], dev(z, c, to, y)))
        return out

    def block(at, size):
        return cols.at[pl.ds(at, size)]

    def to_partner(g, i, yy):
        blk = block(col_at(c, yy, g), 4)
        return remote(blk, blk, ps.at[g, i], pr.at[g, i], me_partner)

    def y_copies(g):
        blk = block(col_at(c, y, g), 4)
        return (
            remote(blk, blk, ys.at[g, 0], yr.at[g, 0], dev(z, c, x, yp)),
            remote(blk, blk, ys.at[g, 1], yr.at[g, 1], dev(z, c, x, ym)),
        )

    def y_forward(g, way):
        if way == 0:
            blk = block(col_at(c, ym, g), 2)
            return remote(blk, blk, ys.at[g, 2], yr.at[g, 2], dev(z, c, x, yp))
        blk = block(col_at(c, yp, g) + 2, 2)
        return remote(blk, blk, ys.at[g, 3], yr.at[g, 3], dev(z, c, x, ym))

    def y_wait(g, i):
        blk = block(col_at(c, y, g), 4 if i < 2 else 2)
        remote(blk, blk, ys.at[g, 0], yr.at[g, i], me_partner).wait_recv()

    def ints_copies():
        return [
            remote(ints, ints_v.at[x], i_sem.at[0, i], i_sem.at[1, i], dev(z, c, (x + d) % 4, y))
            for i, d in enumerate((1, 2, 3))
        ]

    def ens_copies_x():
        return [
            remote(ens, ens_v.at[y, x], e_sem.at[0, i], e_sem.at[1, i], dev(z, c, (x + d) % 4, y))
            for i, d in enumerate((1, 2, 3))
        ]

    def ens_copies_y():
        return [
            remote(ens_v.at[y], ens_v.at[y], e_sem.at[0, 3 + i], e_sem.at[1, 3 + i], dev(z, c, x, (y + d) % 4))
            for i, d in enumerate((1, 2, 3))
        ]

    a_rows = a_v.at[pl.ds(pl.multiple_of(c * PANEL, PANEL), PANEL), :]
    a_partner = remote(fac, a_rows, a_sem.at[0], a_sem.at[1], me_partner)
    a_local = pltpu.make_async_copy(fac, a_rows, a_sem.at[2])
    ints_local = pltpu.make_async_copy(ints, ints_v.at[x], i_sem.at[2, 0])
    ens_local = pltpu.make_async_copy(ens, ens_v.at[y, x], e_sem.at[0, 6])

    def start_own(g):
        for cp in own_copies(g):
            cp.start()
        own_local(g).start()

    start_own(0)
    a_partner.start()
    a_local.start()
    start_own(1)
    for cp in ints_copies() + ens_copies_x():
        cp.start()
    ints_local.start()
    ens_local.start()

    def step(t, carry):
        @pl.when(t < CHUNKS)
        def _():
            z_wait(t, 2 * zm)
            fwd = z_forwards(t)
            fwd[0].start()
            z_wait(t, 2 * zp + 1)
            fwd[1].start()

        @pl.when(t < CHUNKS - 2)
        def _():
            start_own(t + 2)

        @pl.when((t >= 2) & (t < CHUNKS + 2))
        def _():
            g = t - 2
            y_wait(g, 0)
            y_forward(g, 0).start()
            y_wait(g, 1)
            y_forward(g, 1).start()
            to_partner(g, 1, ym).start()
            to_partner(g, 2, yp).start()

        @pl.when(t >= 3)
        def _():
            g = t - 3
            y_wait(g, 2)
            y_wait(g, 3)
            to_partner(g, 3, yo).start()

        @pl.when((t >= 1) & (t < CHUNKS + 1))
        def _():
            g = t - 1

            @pl.when(g == 0)
            def _():
                a_partner.wait_recv()
                a_local.wait()

            own_local(g).wait()
            z_wait(g, 2 * z + nc)
            z_wait(g, 2 * zm + 1)
            z_wait(g, 2 * zp)
            z_wait(g, 2 * zo)
            z_wait(g, 2 * zo + 1)

            def fit(q, carry):
                rows = pl.ds(pl.multiple_of(q * QROWS, QROWS), QROWS)
                acc = jnp.dot(a_v[rows, :], b_v[g], preferred_element_type=F32)
                f_v[g, q] = acc.T.astype(BF16)
                return carry

            lax.fori_loop(0, 4, fit, 0)
            cols[col_at(c, y, g) + x] = f_v[g, x]
            for cp in x_copies(g):
                cp.start()
            for cp in x_copies(g):
                cp.wait_recv()
            for cp in y_copies(g):
                cp.start()
            to_partner(g, 0, y).start()

        return carry

    lax.fori_loop(0, CHUNKS + 3, step, 0)

    for cp in ints_copies() + ens_copies_x():
        cp.wait()
    ints_local.wait()
    ens_local.wait()
    for cp in ens_copies_y():
        cp.start()
    ints_smem = pltpu.make_async_copy(ints_v, ints_s, i_sem.at[2, 1])
    ints_smem.start()
    ints_smem.wait()

    def drain(g, carry):
        for i, yy in enumerate((y, ym, yp, yo)):
            to_partner(g, i, yy).wait()
        for cp in own_copies(g):
            cp.wait_send()
        for cp in z_forwards(g):
            cp.wait_send()
        for cp in x_copies(g):
            cp.wait_send()
        for cp in y_copies(g):
            cp.wait_send()
        for way in (0, 1):
            y_forward(g, way).wait_send()
        return carry

    lax.fori_loop(0, CHUNKS, drain, 0)
    a_partner.wait_send()

    def orbital(xo, position):
        k = ints_s[xo, 1, position]
        t = ints_s[xo, 0, k]
        s = k // 8
        return ((t // 8) * 4 + s % 4) * (CHUNKS * 4) + (t % 8) * 4 + s // 4

    def pairs(half, first):
        def one(i, carry):
            second, slot = i // 4, i % 4
            xo, zo_ = (first, second) if half == 0 else (second, first)
            n = (2 * zo_ + c) * 8 + half * 4 + slot
            left = cols[orbital(xo, 2 * n)]
            right = cols[orbital(xo, 2 * n + 1)]
            e = lax.dot_general(left, right, (((1,), (1,)), ((), ())), preferred_element_type=F32)
            part[half, first, i] = (e * SCALE).astype(BF16)
            return carry

        lax.fori_loop(0, 16, one, 0, unroll=4)

    def rs1_copy(half, d):
        me_at = x if half == 0 else z
        there = (me_at + d) % 4
        to = dev(z, c, there, y) if half == 0 else dev(there, c, x, y)
        return remote(part.at[half, there], rs1.at[half, d - 1], r_sem.at[0, half, d], r_sem.at[1, half, d], to)

    def rs2_copy(half, d):
        me_at = z if half == 0 else x
        there = (me_at + d) % 4
        to = dev(there, c, x, y) if half == 0 else dev(z, c, there, y)
        return remote(summed.at[half, pl.ds(there * 4, 4)], rs2.at[half, d - 1], r_sem.at[2, half, d], r_sem.at[3, half, d], to)

    for d in (2, 1, 3, 0):
        pairs(0, (x + d) % 4)
        pairs(1, (z + d) % 4)
        if d:
            rs1_copy(0, d).start()
            rs1_copy(1, d).start()

    for cp in ens_copies_y():
        cp.wait()
    ens_smem = pltpu.make_async_copy(ens_v, ens_s, e_sem.at[1, 6])
    ens_smem.start()
    ens_smem.wait()
    live = ints_s[x, 2, 0]

    def energy(position):
        k = ints_s[x, 1, position]
        t = ints_s[x, 0, k]
        s = k // 8
        return ens_s[s % 4, s // 4, 0, t]

    for slot in range(8):
        n = f * 8 + slot
        denom = cabs[...] - (energy(2 * n) + energy(2 * n + 1))
        rec_out[pl.ds(slot, 1), :] = jnp.where(n < live, 1.0 / denom, 0.0)

    for half in (0, 1):
        me_at = x if half == 0 else z
        for d in (1, 2, 3):
            rs1_copy(half, d).wait_recv()

        def add(i, carry):
            total = part[half, me_at, i].astype(F32)
            for d in (0, 1, 2):
                total = total + rs1[half, d, i].astype(F32)
            summed[half, i] = total.astype(BF16)
            return carry

        lax.fori_loop(0, 16, add, 0)
        for d in (2, 1, 3):
            rs2_copy(half, d).start()

    for half in (0, 1):
        me_at = z if half == 0 else x
        for d in (1, 2, 3):
            rs2_copy(half, d).wait_recv()

        for i in range(4):
            total = summed[half, me_at * 4 + i].astype(F32)
            for d in (0, 1, 2):
                total = total + rs2[half, d, i].astype(F32)
            exch_out[half * 4 + i] = total.astype(BF16)

    for half in (0, 1):
        for d in (1, 2, 3):
            rs1_copy(half, d).wait_send()
            rs2_copy(half, d).wait_send()


def project_kernel(exch, coupling, rec, out):
    weighted = jnp.dot(exch[0], coupling[...], preferred_element_type=F32)
    out[0] = (weighted * rec[0]).astype(BF16)


def on_device(fac, tri, send_map, pair_slots, pair_count, orbital_energy, cabs_energy, coupling):
    dma = pltpu.SemaphoreType.DMA
    ints = jnp.concatenate(
        [
            send_map.reshape(1, LANES),
            pair_slots,
            jnp.broadcast_to(pair_count[:, None], (6, LANES)),
        ],
        axis=0,
    )
    ens = jnp.broadcast_to(jnp.pad(orbital_energy.astype(F32), (0, LANES - 16))[None, :], (8, LANES))
    hbm = pl.BlockSpec(memory_space=pl.ANY)
    vmem = pl.BlockSpec(memory_space=pltpu.VMEM)
    exch, rec = pl.pallas_call(
        fused_kernel,
        out_shape=(
            jax.ShapeDtypeStruct((8, LANES, LANES), BF16),
            jax.ShapeDtypeStruct((8, 1024), F32),
        ),
        in_specs=[hbm, hbm, hbm, hbm, vmem],
        out_specs=(vmem, vmem),
        scratch_shapes=[
            pltpu.VMEM((2 * PANEL, 4096), BF16),
            pltpu.VMEM((CHUNKS, 4096, LANES), BF16),
            pltpu.VMEM((CHUNKS, 4, LANES, QROWS), BF16),
            pltpu.VMEM((256, LANES, QROWS), BF16),
            pltpu.VMEM((2, 4, 16, LANES, LANES), BF16),
            pltpu.VMEM((2, 3, 16, LANES, LANES), BF16),
            pltpu.VMEM((2, 16, LANES, LANES), BF16),
            pltpu.VMEM((2, 3, 4, LANES, LANES), BF16),
            pltpu.VMEM((4, 8, LANES), jnp.int32),
            pltpu.VMEM((4, 4, 8, LANES), F32),
            pltpu.SMEM((4, 8, LANES), jnp.int32),
            pltpu.SMEM((4, 4, 8, LANES), F32),
            dma((3,)),
            dma((CHUNKS, 7)),
            dma((CHUNKS, 8)),
            dma((CHUNKS, 3)),
            dma((CHUNKS, 3)),
            dma((CHUNKS, 4)),
            dma((CHUNKS, 4)),
            dma((CHUNKS, 4)),
            dma((CHUNKS, 4)),
            dma((3, 3)),
            dma((2, 7)),
            dma((4, 2, 4)),
            dma((CHUNKS,)),
        ],
        compiler_params=pltpu.CompilerParams(
            collective_id=0, has_side_effects=True, vmem_limit_bytes=64 * 1024 * 1024 - 65536
        ),
        name="fit_exchange",
    )(fac, tri, ints, ens, cabs_energy.reshape(1, 1024))
    projected = pl.pallas_call(
        project_kernel,
        grid=(8,),
        out_shape=jax.ShapeDtypeStruct((8, LANES, 1024), BF16),
        in_specs=[
            pl.BlockSpec((1, LANES, LANES), lambda i: (i, 0, 0)),
            pl.BlockSpec((LANES, 1024), lambda i: (0, 0)),
            pl.BlockSpec((1, 1, 1024), lambda i: (i, 0, 0)),
        ],
        out_specs=pl.BlockSpec((1, LANES, 1024), lambda i: (i, 0, 0)),
        name="project",
    )(exch, coupling, rec.reshape(8, 1, 1024))
    return projected.reshape(1, 8, LANES, 1024)


def solution(mesh):
    in_specs = (
        P("fit", None),
        P("fit", "pair"),
        P("pair", None, None),
        P("pair", None),
        P("pair"),
        P("pair"),
        P(),
        P(),
    )
    return jax.shard_map(
        on_device, mesh=mesh, in_specs=in_specs, out_specs=P("pair", "fit", None, None), check_vma=False
    )
```

time: 510 us -> 193 us (0.38)
  waiting for transfers between devices: 335 us -> 0 us
  Pallas kernels: 0 us -> 187 us
  local copies, waits for them, and re-layouts: 133 us -> 2.91 us
  matrix products: 21.7 us -> 0 us
  between operations: 13.9 us -> 0.67 us
    all_gather x2 -> x0, waiting for transfers between devices: 284 us -> none  [the longest x1 195 us: turned_gather(): filled, at, outs = (lax.all_gather(both, axis, axis=0, tiled=True), 0, [])]
    pallas_call x0 -> x2, Pallas kernels: none -> 187 us  [the longest x1 181 us: on_device(): pl.pallas_call(fused_kernel, out_shape=(jax.ShapeDtypeStruct((8, LANES, L...]
    slice x5 -> x0, local copies, waits for them, and re-layouts: 65.7 us -> none  [the longest x3 65.4 us: turned_gather(): slab = filled[:, at:at + t[0].size].reshape(-1, *t.shape[1:])]
    reduce_scatter x1 -> x0, waiting for transfers between devices: 49.6 us -> none  [on_device(): lax.psum_scatter(partial_value.astype(jnp.bfloat16), 'fit', scatter_dimen...]
    while x1 -> x0, local copies, waits for them, and re-layouts: 43.8 us -> none  [on_device(): partial_value = lax.fori_loop(0, block_count, advance, partial_value)]
    dot_general x6 -> x0, matrix products: 21.7 us -> none  [the longest x1 13.6 us: on_device(): jnp.dot(metric_factor, lax.all_gather(three_index, 'fit', axis=0, tiled=T...]
    gather x11 -> x0, local copies, waits for them, and re-layouts: 18.5 us -> none  [the longest x4 7.84 us: advance(): left_rows = jnp.take(source, left_ids, axis=1)]
  transfers between devices with their start and end apart: 3 -> 0, of which waited for: 3 -> 0; matrix products, arithmetic and copies ran while one was open for 1% -> 0% of each run, Pallas kernels for 0% -> 0%
where the time goes in v1:
time: 193 us; the launch traced here: 192 us
  Pallas kernels  187 us (97%)
  local copies, waits for them, and re-layouts  2.91 us (2%)
  other arithmetic  1.98 us (1%)
    pallas_call x1, Pallas kernels, on_device(): pl.pallas_call(fused_kernel, out_shape=(jax.ShapeDtypeStruct((8, LANES, L...  181 us
    pallas_call x1, Pallas kernels, on_device(): pl.pallas_call(project_kernel, grid=(8,), out_shape=jax.ShapeDtypeStruct(...  5.68 us

profile of v1, /device:TPU:1, one launch (start us, length us, event | category | flops | bytes accessed | tf_op | source)
XLA Modules:
  0.0 192.5 jit_solution(16383873261381099567)
XLA Ops:
  0.7 0.1 pad.11.clone
  0.7 0.7 pad_convert_fusion
  1.4 0.6 broadcast_in_dim.16.ens
  2.0 0.8 copy.10
  2.7 0.1 reshape.14
  2.8 1.3 add_add_fusion.ints
  4.2 181.2 %fit_exchange.1 = (bf16[8,128,128]{2,1,0:T(8,128)(2,1)}, f32[8,1024]{1,0:T(8,128)}) custom-call(bf16[512,4096]{1,0:T(8,128)(2,1)} %fac.1, bf16[512,2048]{1,0:T(8,128)(2,1)} %tri.1, s32[8,128]{1,0:T(8,128)} %add_add_fusion.ints, f32[8,128]{1,0:T(8,128)} %broadcast_in_dim.16.ens, f32[1,1024]{1,0:T(1,128)} %bitcast.4), custom_call_target="tpu_custom_call" | custom-call | tf_op jit(solution)/shard_map/fit_exchange/pallas_call | solution.py:353
  185.4 1.4 reshape.16.rec
  186.8 5.7 %project.1 = bf16[8,128,1024]{2,1,0:T(8,128)(2,1)} custom-call(bf16[8,128,128]{2,1,0:T(8,128)(2,1)} %get-tuple-element.7.exch, bf16[128,1024]{1,0:T(8,128)(2,1)} %coupling.1, f32[8,1,1024]{2,1,0:T(1,128)} %reshape.16.rec), custom_call_target="tpu_custom_call" | custom-call | tf_op jit(solution)/shard_map/project/pallas_call | solution.py:393
  (1 shorter events, 0.0 us)

commit v2 on v1

v2 whole, which is shorter than its diff:
```python
import jax
import jax.numpy as jnp
from jax import lax
from jax.experimental import pallas as pl
from jax.experimental.pallas import tpu as pltpu
from jax.sharding import PartitionSpec as P

MESH = pl.DeviceIdType.MESH
F32 = jnp.float32
BF16 = jnp.bfloat16
CHUNKS = 8
LANES = 128
PANEL = 512
QROWS = 256
SCALE = 4096.0 ** -0.5


def fused_kernel(
    fac, tri, wanted, slots, ens, cabs, count,
    exch_out, rec_out,
    a_v, b_v, f_v, cols, part, rs_far, rs_near, summed, rs2,
    wanted_v, slots_v, ens_v, wanted_s, slots_s, ens_s,
    a_sem, zs, zr, xs, xr, ys, yr, ps, pr, i_sem, e_sem, r_sem, l_sem,
):
    f = lax.axis_index("fit")
    p = lax.axis_index("pair")
    z, c = f // 2, f % 2
    x, y = p // 4, p % 4
    nc = 1 - c
    zp, zm, zo = (z + 1) % 4, (z + 3) % 4, (z + 2) % 4
    yp, ym, yo = (y + 1) % 4, (y + 3) % 4, (y + 2) % 4

    def dev(zz, cc, xx, yy):
        return (2 * zz + cc, 4 * xx + yy)

    me_partner = dev(z, nc, x, y)

    def remote(src, dst, ss, rs, to):
        return pltpu.make_async_remote_copy(
            src_ref=src, dst_ref=dst, send_sem=ss, recv_sem=rs, device_id=to, device_id_type=MESH
        )

    barrier = pltpu.get_barrier_semaphore()
    greeted = [me_partner]
    for d in (1, 2, 3):
        greeted.append(dev((z + d) % 4, c, x, y))
        greeted.append(dev(z, c, (x + d) % 4, y))
        greeted.append(dev(z, c, x, (y + d) % 4))
    greeted.append(dev(zp, nc, x, y))
    greeted.append(dev(zm, nc, x, y))
    for to in greeted:
        pl.semaphore_signal(barrier, inc=1, device_id=to, device_id_type=MESH)
    pl.semaphore_wait(barrier, len(greeted))

    def own_src(h, g):
        return tri.at[:, pl.ds(pl.multiple_of((h * CHUNKS + g) * LANES, LANES), LANES)]

    def panel(g, k):
        return b_v.at[g, pl.ds(pl.multiple_of(k * PANEL, PANEL), PANEL), :]

    def own_copies(g):
        out = []
        for i, (zz, h) in enumerate(((zp, 0), (zm, 0), (zp, 1), (zm, 1))):
            out.append(remote(own_src(h, g), panel(g, f), zs.at[g, i], zr.at[g, f], dev(zz, h, x, y)))
        out.append(remote(own_src(nc, g), panel(g, f), zs.at[g, 4], zr.at[g, f], me_partner))
        return out

    def own_local(g):
        return pltpu.make_async_copy(own_src(c, g), panel(g, f), l_sem.at[g])

    def z_wait(g, k):
        remote(panel(g, k), panel(g, k), zs.at[g, 0], zr.at[g, k], me_partner).wait_recv()

    def z_forwards(g):
        return (
            remote(panel(g, 2 * zm), panel(g, 2 * zm), zs.at[g, 5], zr.at[g, 2 * zm], dev(zp, c, x, y)),
            remote(panel(g, 2 * zp + 1), panel(g, 2 * zp + 1), zs.at[g, 6], zr.at[g, 2 * zp + 1], dev(zm, c, x, y)),
        )

    def col_at(cc, yy, g):
        return ((cc * 4 + yy) * CHUNKS + g) * 4

    def x_copy(g, i):
        to = (x + 3 - i) % 4
        return remote(f_v.at[g, to], cols.at[col_at(c, y, g) + x], xs.at[g, i], xr.at[g, i], dev(z, c, to, y))

    def x_wait(g, i):
        at = cols.at[col_at(c, y, g)]
        remote(at, at, xs.at[g, 0], xr.at[g, i], me_partner).wait_recv()

    def block(at, size):
        return cols.at[pl.ds(at, size)]

    def to_partner(g, i, yy):
        blk = block(col_at(c, yy, g), 4)
        return remote(blk, blk, ps.at[g, i], pr.at[g, i], me_partner)

    def y_copies(g):
        blk = block(col_at(c, y, g), 4)
        return (
            remote(blk, blk, ys.at[g, 0], yr.at[g, 0], dev(z, c, x, yp)),
            remote(blk, blk, ys.at[g, 1], yr.at[g, 1], dev(z, c, x, ym)),
        )

    def y_forward(g, way):
        if way == 0:
            blk = block(col_at(c, ym, g), 2)
            return remote(blk, blk, ys.at[g, 2], yr.at[g, 2], dev(z, c, x, yp))
        blk = block(col_at(c, yp, g) + 2, 2)
        return remote(blk, blk, ys.at[g, 3], yr.at[g, 3], dev(z, c, x, ym))

    def y_wait(g, i):
        blk = block(col_at(c, y, g), 4 if i < 2 else 2)
        remote(blk, blk, ys.at[g, 0], yr.at[g, i], me_partner).wait_recv()

    def ints_copies():
        out = []
        for i, d in enumerate((1, 2, 3)):
            to = dev(z, c, (x + d) % 4, y)
            out.append(remote(wanted.at[0], wanted_v.at[x], i_sem.at[0, i], i_sem.at[1, i], to))
            out.append(remote(slots, slots_v.at[x], i_sem.at[2, i], i_sem.at[3, i], to))
        return out

    def ens_copies_x():
        return [
            remote(ens, ens_v.at[y, x], e_sem.at[0, i], e_sem.at[1, i], dev(z, c, (x + d) % 4, y))
            for i, d in enumerate((1, 2, 3))
        ]

    def ens_copies_y():
        return [
            remote(ens_v.at[y], ens_v.at[y], e_sem.at[0, 3 + i], e_sem.at[1, 3 + i], dev(z, c, x, (y + d) % 4))
            for i, d in enumerate((1, 2, 3))
        ]

    a_rows = a_v.at[pl.ds(pl.multiple_of(c * PANEL, PANEL), PANEL), :]
    a_partner = remote(fac, a_rows, a_sem.at[0], a_sem.at[1], me_partner)
    a_local = pltpu.make_async_copy(fac, a_rows, a_sem.at[2])
    small_local = (
        pltpu.make_async_copy(wanted.at[0], wanted_v.at[x], i_sem.at[0, 3]),
        pltpu.make_async_copy(slots, slots_v.at[x], i_sem.at[1, 3]),
        pltpu.make_async_copy(ens, ens_v.at[y, x], e_sem.at[0, 6]),
    )

    def start_own(g):
        for cp in own_copies(g):
            cp.start()
        own_local(g).start()

    start_own(0)
    a_partner.start()
    a_local.start()
    for cp in ints_copies() + ens_copies_x():
        cp.start()
    for cp in small_local:
        cp.start()

    def step(t, carry):
        @pl.when(t < CHUNKS)
        def _():
            z_wait(t, 2 * zm)
            fwd = z_forwards(t)
            fwd[0].start()
            z_wait(t, 2 * zp + 1)
            fwd[1].start()

        @pl.when(t == 0)
        def _():
            start_own(1)

        @pl.when(t < CHUNKS - 2)
        def _():
            start_own(t + 2)

        @pl.when((t == 1) | ((t >= 3) & (t < CHUNKS + 2)))
        def _():
            g = jnp.maximum(t - 2, 0)
            for i in range(3):
                x_wait(g, i)
            for cp in y_copies(g):
                cp.start()
            to_partner(g, 0, y).start()

        @pl.when((t == 0) | ((t >= 2) & (t < CHUNKS + 1)))
        def _():
            g = jnp.maximum(t - 1, 0)

            @pl.when(g == 0)
            def _():
                a_partner.wait_recv()
                a_local.wait()

            own_local(g).wait()
            z_wait(g, 2 * z + nc)
            z_wait(g, 2 * zm + 1)
            z_wait(g, 2 * zp)
            z_wait(g, 2 * zo)
            z_wait(g, 2 * zo + 1)

            def fit(q):
                rows = pl.ds(pl.multiple_of(q * QROWS, QROWS), QROWS)
                acc = jnp.dot(a_v[rows, :], b_v[g], preferred_element_type=F32)
                return acc.T.astype(BF16)

            def fit_send(i, carry):
                q = (x + 3 - i) % 4
                f_v[g, q] = fit(q)
                x_copy(g, i).start()
                return carry

            lax.fori_loop(0, 3, fit_send, 0)
            cols[col_at(c, y, g) + x] = fit(x)

        @pl.when((t >= 3) & (t < CHUNKS + 3))
        def _():
            g = t - 3
            y_wait(g, 0)
            y_forward(g, 0).start()
            y_wait(g, 1)
            y_forward(g, 1).start()
            to_partner(g, 1, ym).start()
            to_partner(g, 2, yp).start()

        @pl.when(t >= 4)
        def _():
            g = t - 4
            y_wait(g, 2)
            y_wait(g, 3)
            to_partner(g, 3, yo).start()

        @pl.when(t == 2)
        def _():
            for cp in ints_copies() + ens_copies_x():
                cp.wait()
            for cp in small_local:
                cp.wait()
            for cp in ens_copies_y():
                cp.start()

        @pl.when(t == 6)
        def _():
            for cp in ens_copies_y():
                cp.wait()
            to_smem = (
                pltpu.make_async_copy(wanted_v, wanted_s, i_sem.at[2, 3]),
                pltpu.make_async_copy(slots_v, slots_s, i_sem.at[3, 3]),
                pltpu.make_async_copy(ens_v, ens_s, e_sem.at[1, 6]),
            )
            for cp in to_smem:
                cp.start()
            for cp in to_smem:
                cp.wait()

        return carry

    lax.fori_loop(0, CHUNKS + 4, step, 0)

    def drain(g, carry):
        for i, yy in enumerate((y, ym, yp, yo)):
            to_partner(g, i, yy).wait()
        for cp in own_copies(g):
            cp.wait_send()
        for cp in z_forwards(g):
            cp.wait_send()
        for i in range(3):
            x_copy(g, i).wait_send()
        for cp in y_copies(g):
            cp.wait_send()
        for way in (0, 1):
            y_forward(g, way).wait_send()
        return carry

    lax.fori_loop(0, CHUNKS, drain, 0)
    a_partner.wait_send()

    def orbital(xo, position):
        k = slots_s[xo, 0, position]
        s = k >> 3
        t = wanted_s[xo, s, k & 7]
        return ((t >> 3) << 7) + ((s & 3) << 5) + ((t & 7) << 2) + (s >> 2)

    def pairs(half, first):
        def some(j, carry):
            done = []
            for slot in range(8):
                second = 2 * j + slot // 4
                xo, zz = (first, second) if half == 0 else (second, first)
                n = (2 * zz + c) * 8 + half * 4 + slot % 4
                left = cols[orbital(xo, 2 * n)]
                right = cols[orbital(xo, 2 * n + 1)]
                e = lax.dot_general(left, right, (((1,), (1,)), ((), ())), preferred_element_type=F32)
                done.append((e * SCALE).astype(BF16))
            for slot in range(8):
                part[half, first, j * 8 + slot] = done[slot]
            return carry

        lax.fori_loop(0, 2, some, 0)

    def ring(half, d):
        if half == 0:
            at = (x + d) % 4
            return at, dev(z, c, at, y)
        at = (z + d) % 4
        return at, dev(at, c, x, y)

    def far_copy(half, i):
        far, _ = ring(half, 2)
        _, to = ring(half, 3 if i == 0 else 1)
        return remote(part.at[half, far, pl.ds(8 * i, 8)], rs_far.at[half, i], r_sem.at[0, half, i], r_sem.at[1, half, i], to)

    def near_copy(half, i, summed_part):
        at, to = ring(half, 3 if i == 0 else 1)
        first = 8 * i if summed_part else 8 - 8 * i
        j = 2 * i + (1 if summed_part else 0)
        rows = pl.ds(first, 8)
        return remote(part.at[half, at, rows], rs_near.at[half, i, rows], r_sem.at[2, half, j], r_sem.at[3, half, j], to)

    def combine(half, i):
        at, _ = ring(half, 3 if i == 0 else 1)
        far_copy(half, i).wait_recv()

        def add(k, carry):
            part[half, at, 8 * i + k] = (part[half, at, 8 * i + k].astype(F32) + rs_far[half, i, k].astype(F32)).astype(BF16)
            return carry

        lax.fori_loop(0, 8, add, 0, unroll=2)

    def rs2_copy(half, d):
        there, to = ring(1 - half, d)
        return remote(summed.at[half, pl.ds(there * 4, 4)], rs2.at[half, d - 1], r_sem.at[4, half, d], r_sem.at[5, half, d], to)

    pairs(0, ring(0, 2)[0])
    pairs(1, ring(1, 2)[0])
    for i in (0, 1):
        far_copy(0, i).start()
        far_copy(1, i).start()
    for i, d in ((0, 3), (1, 1)):
        pairs(0, ring(0, d)[0])
        pairs(1, ring(1, d)[0])
        near_copy(0, i, False).start()
        near_copy(1, i, False).start()
    pairs(0, x)
    pairs(1, z)
    for half in (0, 1):
        for i in (0, 1):
            combine(half, i)
            near_copy(half, i, True).start()

    live = count[0]

    def energy(position):
        k = slots_s[x, 0, position]
        s = k >> 3
        return ens_s[s & 3, s >> 2, 0, wanted_s[x, s, k & 7]]

    for slot in range(8):
        n = f * 8 + slot
        denom = cabs[...] - (energy(2 * n) + energy(2 * n + 1))
        rec_out[slot] = jnp.where(n < live, 1.0 / denom, 0.0)

    for half in (0, 1):
        me_at = x if half == 0 else z
        for i in (0, 1):
            near_copy(half, i, False).wait_recv()
            near_copy(half, i, True).wait_recv()

        def add(i, carry):
            total = part[half, me_at, i].astype(F32)
            for d in (0, 1):
                total = total + rs_near[half, d, i].astype(F32)
            summed[half, i] = total.astype(BF16)
            return carry

        lax.fori_loop(0, 16, add, 0, unroll=2)
        for d in (2, 1, 3):
            rs2_copy(half, d).start()

    for half in (0, 1):
        me_at = z if half == 0 else x
        for d in (1, 2, 3):
            rs2_copy(half, d).wait_recv()

        for i in range(4):
            total = summed[half, me_at * 4 + i].astype(F32)
            for d in (0, 1, 2):
                total = total + rs2[half, d, i].astype(F32)
            exch_out[half * 4 + i] = total.astype(BF16)

    for half in (0, 1):
        for i in (0, 1):
            far_copy(half, i).wait_send()
            near_copy(half, i, False).wait_send()
            near_copy(half, i, True).wait_send()
        for d in (1, 2, 3):
            rs2_copy(half, d).wait_send()


def project_kernel(exch, coupling, rec, out):
    weighted = jnp.dot(exch[0], coupling[...], preferred_element_type=F32)
    out[0] = (weighted * rec[0]).astype(BF16)


def on_device(fac, tri, send_map, pair_slots, pair_count, orbital_energy, cabs_energy, coupling):
    dma = pltpu.SemaphoreType.DMA
    ens = jnp.broadcast_to(orbital_energy.astype(F32)[None, :], (8, 16))
    hbm = pl.BlockSpec(memory_space=pl.ANY)
    vmem = pl.BlockSpec(memory_space=pltpu.VMEM)
    exch, rec = pl.pallas_call(
        fused_kernel,
        out_shape=(
            jax.ShapeDtypeStruct((8, LANES, LANES), BF16),
            jax.ShapeDtypeStruct((8, 1, 1024), F32),
        ),
        in_specs=[hbm, hbm, hbm, hbm, hbm, vmem, pl.BlockSpec(memory_space=pltpu.SMEM)],
        out_specs=(vmem, vmem),
        scratch_shapes=[
            pltpu.VMEM((2 * PANEL, 4096), BF16),
            pltpu.VMEM((CHUNKS, 4096, LANES), BF16),
            pltpu.VMEM((CHUNKS, 4, LANES, QROWS), BF16),
            pltpu.VMEM((256, LANES, QROWS), BF16),
            pltpu.VMEM((2, 4, 16, LANES, LANES), BF16),
            pltpu.VMEM((2, 2, 8, LANES, LANES), BF16),
            pltpu.VMEM((2, 2, 16, LANES, LANES), BF16),
            pltpu.VMEM((2, 16, LANES, LANES), BF16),
            pltpu.VMEM((2, 3, 4, LANES, LANES), BF16),
            pltpu.VMEM((4, 16, 8), jnp.int32),
            pltpu.VMEM((4, 1, LANES), jnp.int32),
            pltpu.VMEM((4, 4, 8, 16), F32),
            pltpu.SMEM((4, 16, 8), jnp.int32),
            pltpu.SMEM((4, 1, LANES), jnp.int32),
            pltpu.SMEM((4, 4, 8, 16), F32),
            dma((3,)),
            dma((CHUNKS, 7)),
            dma((CHUNKS, 8)),
            dma((CHUNKS, 3)),
            dma((CHUNKS, 3)),
            dma((CHUNKS, 4)),
            dma((CHUNKS, 4)),
            dma((CHUNKS, 4)),
            dma((CHUNKS, 4)),
            dma((4, 4)),
            dma((2, 7)),
            dma((6, 2, 4)),
            dma((CHUNKS,)),
        ],
        compiler_params=pltpu.CompilerParams(
            collective_id=0, has_side_effects=True, vmem_limit_bytes=64 * 1024 * 1024 - 65536
        ),
        name="fit_exchange",
    )(fac, tri, send_map, pair_slots, ens, cabs_energy.reshape(1, 1024), pair_count)
    projected = pl.pallas_call(
        project_kernel,
        grid=(8,),
        out_shape=jax.ShapeDtypeStruct((8, LANES, 1024), BF16),
        in_specs=[
            pl.BlockSpec((1, LANES, LANES), lambda i: (i, 0, 0)),
            pl.BlockSpec((LANES, 1024), lambda i: (0, 0)),
            pl.BlockSpec((1, 1, 1024), lambda i: (i, 0, 0)),
        ],
        out_specs=pl.BlockSpec((1, LANES, 1024), lambda i: (i, 0, 0)),
        name="project",
    )(exch, coupling, rec)
    return projected.reshape(1, 8, LANES, 1024)


def solution(mesh):
    in_specs = (
        P("fit", None),
        P("fit", "pair"),
        P("pair", None, None),
        P("pair", None),
        P("pair"),
        P("pair"),
        P(),
        P(),
    )
    return jax.shard_map(
        on_device, mesh=mesh, in_specs=in_specs, out_specs=P("pair", "fit", None, None), check_vma=False
    )
```

time: 193 us -> 148 us (0.77)
  Pallas kernels: 187 us -> 144 us
  other arithmetic: 1.98 us -> 0 us
    pallas_call x1, Pallas kernels: 181 us -> 139 us  [on_device(): pl.pallas_call(fused_kernel, out_shape=(jax.ShapeDtypeStruct((8, LANES, L...]
where the time goes in v2:
time: 148 us
  Pallas kernels  144 us (97%)
  local copies, waits for them, and re-layouts  2.6 us (2%)
    pallas_call x1, Pallas kernels, on_device(): pl.pallas_call(fused_kernel, out_shape=(jax.ShapeDtypeStruct((8, LANES, L...  139 us
    pallas_call x1, Pallas kernels, on_device(): pl.pallas_call(project_kernel, grid=(8,), out_shape=jax.ShapeDtypeStruct(...  5.71 us

profile of v2, /device:TPU:1, one launch (start us, length us, event | category | flops | bytes accessed | tf_op | source)
XLA Modules:
  0.0 147.5 jit_solution(18221709103640921853)
XLA Ops:
  0.7 1.2 broadcast_in_dim.2.ens
  1.9 1.4 copy.9.wanted
  3.3 138.6 %fit_exchange.1 = (bf16[8,128,128]{2,1,0:T(8,128)(2,1)}, f32[8,1,1024]{2,1,0:T(1,128)}) custom-call(bf16[512,4096]{1,0:T(8,128)(2,1)} %fac.1, bf16[512,2048]{1,0:T(8,128)(2,1)} %tri.1, s32[1,16,8]{2,1,0:T(8,128)} %copy.9.wanted, s32[1,128]{1,0:T(1,128)} %slots.1, f32[8,16]{1,0:T(8,128)} %broadcast_in_dim.2.ens, f32[1,1024]{1,0:T(1,128)} %bitcast.2, ...), custom_call_target="tpu_custom_call" | custom-call | tf_op jit(solution)/shard_map/fit_exchange/pallas_call | solution.py:408
  141.8 5.7 %project.1 = bf16[8,128,1024]{2,1,0:T(8,128)(2,1)} custom-call(bf16[8,128,128]{2,1,0:T(8,128)(2,1)} %get-tuple-element.7.exch, bf16[128,1024]{1,0:T(8,128)(2,1)} %coupling.1, f32[8,1,1024]{2,1,0:T(1,128)} %get-tuple-element.8.rec), custom_call_target="tpu_custom_call" | custom-call | tf_op jit(solution)/shard_map/project/pallas_call | solution.py:451

commit v3 on v2

v3 whole, which is shorter than its diff:
```python
import jax
import jax.numpy as jnp
from jax import lax
from jax.experimental import pallas as pl
from jax.experimental.pallas import tpu as pltpu
from jax.sharding import PartitionSpec as P

MESH = pl.DeviceIdType.MESH
F32 = jnp.float32
BF16 = jnp.bfloat16
CHUNKS = 8
LANES = 128
PANEL = 512
QROWS = 256
SCALE = 4096.0 ** -0.5


def fused_kernel(
    fac, tri, wanted, slots, ens, cabs, coupling, count,
    out,
    a_v, b_v, f_v, cols, part, rs_far, rs_near, summed, rs2,
    wanted_v, slots_v, ens_v, wanted_s, slots_s, ens_s, rec_v, out_v,
    send_sem, a_sem, zr, xr, yr, pr, i_sem, e_sem, r_sem, l_sem, o_sem,
):
    f = lax.axis_index("fit")
    p = lax.axis_index("pair")
    z, c = f // 2, f % 2
    x, y = p // 4, p % 4
    nc = 1 - c
    zp, zm, zo = (z + 1) % 4, (z + 3) % 4, (z + 2) % 4
    yp, ym, yo = (y + 1) % 4, (y + 3) % 4, (y + 2) % 4

    def dev(zz, cc, xx, yy):
        return (2 * zz + cc, 4 * xx + yy)

    me_partner = dev(z, nc, x, y)

    def remote(src, dst, ss, rs, to):
        return pltpu.make_async_remote_copy(
            src_ref=src, dst_ref=dst, send_sem=ss, recv_sem=rs, device_id=to, device_id_type=MESH
        )

    barrier = pltpu.get_barrier_semaphore()
    greeted = [me_partner]
    for d in (1, 2, 3):
        greeted.append(dev((z + d) % 4, c, x, y))
        greeted.append(dev(z, c, (x + d) % 4, y))
        greeted.append(dev(z, c, x, (y + d) % 4))
    greeted.append(dev(zp, nc, x, y))
    greeted.append(dev(zm, nc, x, y))
    for to in greeted:
        pl.semaphore_signal(barrier, inc=1, device_id=to, device_id_type=MESH)

    def own_src(h, g):
        return tri.at[:, pl.ds(pl.multiple_of((h * CHUNKS + g) * LANES, LANES), LANES)]

    def panel(g, k):
        return b_v.at[g, pl.ds(pl.multiple_of(k * PANEL, PANEL), PANEL), :]

    def own_first(g):
        return (
            remote(own_src(c, g), panel(g, f), send_sem.at[0], zr.at[g, 0], dev(zp, c, x, y)),
            remote(own_src(c, g), panel(g, f), send_sem.at[0], zr.at[g, 2], dev(zm, c, x, y)),
        )

    def own_second(g):
        return (
            remote(own_src(nc, g), panel(g, f), send_sem.at[0], zr.at[g, 2], dev(zp, nc, x, y)),
            remote(own_src(nc, g), panel(g, f), send_sem.at[0], zr.at[g, 1], dev(zm, nc, x, y)),
            remote(own_src(nc, g), panel(g, f), send_sem.at[0], zr.at[g, 2], me_partner),
        )

    def start(copies):
        for cp in copies:
            cp.start()

    def own_local(g):
        return pltpu.make_async_copy(own_src(c, g), panel(g, f), l_sem)

    def z_forward(g, way):
        k = 2 * zm + c if way == 0 else 2 * zp + nc
        return remote(panel(g, k), panel(g, k), send_sem.at[0], zr.at[g, 2], dev(zp if way == 0 else zm, c, x, y))

    def z_wait(g, i):
        blk = b_v.at[g, pl.ds(0, PANEL if i < 2 else 5 * PANEL), :]
        remote(blk, blk, send_sem.at[0], zr.at[g, i], me_partner).wait_recv()

    def col_at(cc, yy, g):
        return ((cc * 4 + yy) * CHUNKS + g) * 4

    def x_copy(g, i):
        to = (x + 3 - i) % 4
        return remote(f_v.at[g, to], cols.at[col_at(c, y, g) + x], send_sem.at[1], xr.at[g, i], dev(z, c, to, y))

    def x_wait(g, i):
        at = cols.at[col_at(c, y, g)]
        remote(at, at, send_sem.at[1], xr.at[g, i], me_partner).wait_recv()

    def block(at, size):
        return cols.at[pl.ds(at, size)]

    def to_partner(g, yy):
        blk = block(col_at(c, yy, g), 4)
        return remote(blk, blk, send_sem.at[3], pr, me_partner)

    def y_copy(g, way, i):
        blk = cols.at[col_at(c, y, g) + (x + 1 + i) % 4]
        j = ((4, 1, 4, 0), (2, 5, 3, 5))[way][i]
        return remote(blk, blk, send_sem.at[2], yr.at[g, j], dev(z, c, x, yp if way == 0 else ym))

    def y_start(g, i):
        y_copy(g, 0, i).start()
        y_copy(g, 1, i).start()

    def y_forward(g, i):
        yy, to = (ym, yp) if i % 2 else (yp, ym)
        blk = cols.at[col_at(c, yy, g) + (x + 1 + i) % 4]
        return remote(blk, blk, send_sem.at[2], yr.at[g, 6], dev(z, c, x, to))

    def y_wait(g, j):
        blk = block(col_at(c, y, g), (1, 1, 1, 1, 2, 2, 4)[j])
        remote(blk, blk, send_sem.at[2], yr.at[g, j], me_partner).wait_recv()

    def ints_copies():
        out = []
        for i, d in enumerate((1, 2, 3)):
            to = dev(z, c, (x + d) % 4, y)
            out.append(remote(wanted.at[0], wanted_v.at[x], i_sem.at[0, i], i_sem.at[1, i], to))
            out.append(remote(slots, slots_v.at[x], i_sem.at[2, i], i_sem.at[3, i], to))
        return out

    def ens_copies_x():
        return [
            remote(ens, ens_v.at[y, x], e_sem.at[0, i], e_sem.at[1, i], dev(z, c, (x + d) % 4, y))
            for i, d in enumerate((1, 2, 3))
        ]

    def ens_copies_y():
        return [
            remote(ens_v.at[y], ens_v.at[y], e_sem.at[0, 3 + i], e_sem.at[1, 3 + i], dev(z, c, x, (y + d) % 4))
            for i, d in enumerate((1, 2, 3))
        ]

    a_rows = a_v.at[pl.ds(pl.multiple_of(c * PANEL, PANEL), PANEL), :]
    a_partner = remote(fac, a_rows, a_sem.at[0], a_sem.at[1], me_partner)
    a_local = pltpu.make_async_copy(fac, a_rows, a_sem.at[2])
    small_local = (
        pltpu.make_async_copy(wanted.at[0], wanted_v.at[x], i_sem.at[0, 3]),
        pltpu.make_async_copy(slots, slots_v.at[x], i_sem.at[1, 3]),
        pltpu.make_async_copy(ens, ens_v.at[y, x], e_sem.at[0, 6]),
    )

    for g in range(CHUNKS):
        own_local(g).start()
    a_local.start()
    for cp in small_local:
        cp.start()

    pl.semaphore_wait(barrier, len(greeted))

    @pl.when(c == 0)
    def _():
        start(own_first(0))
        start(own_second(0))

    @pl.when(c == 1)
    def _():
        start(own_second(0))
        start(own_first(0))

    a_partner.start()
    for cp in ints_copies() + ens_copies_x():
        cp.start()

    def step(t, carry):
        @pl.when(t < CHUNKS)
        def _():
            z_wait(t, 0)
            z_forward(t, 0).start()
            z_wait(t, 1)
            z_forward(t, 1).start()

        @pl.when(c == 0)
        def _():
            @pl.when(t == 0)
            def _():
                start(own_first(1))

            @pl.when(t < CHUNKS - 1)
            def _():
                start(own_second(t + 1))

            @pl.when(t < CHUNKS - 2)
            def _():
                start(own_first(t + 2))

        @pl.when(c == 1)
        def _():
            @pl.when(t == 0)
            def _():
                start(own_second(1))

            @pl.when(t < CHUNKS - 1)
            def _():
                start(own_first(t + 1))

            @pl.when(t < CHUNKS - 2)
            def _():
                start(own_second(t + 2))

        def send_rest(g):
            for i in (0, 2, 1):
                x_wait(g, i)
                y_start(g, i)
            to_partner(g, y).start()

        @pl.when((t == 1) | ((t >= 3) & (t < CHUNKS)))
        def _():
            send_rest(jnp.maximum(t - 2, 0))

        @pl.when((t == 0) | ((t >= 2) & (t < CHUNKS + 1)))
        def _():
            g = jnp.maximum(t - 1, 0)

            @pl.when(t == 0)
            def _():
                a_partner.wait_recv()
                a_local.wait()
                pltpu.make_async_copy(b_v.at[0], b_v.at[0], l_sem).wait()

            z_wait(g, 2)

            def fit(q):
                rows = pl.ds(pl.multiple_of(q * QROWS, QROWS), QROWS)
                acc = jnp.dot(a_v[rows, :], b_v[g], preferred_element_type=F32)
                return acc.T.astype(BF16)

            cols[col_at(c, y, g) + x] = fit(x)

            def fit_send(j, carry):
                i = jnp.where(j < 2, 1 - j, 2)
                q = (x + 3 - i) % 4
                f_v[g, q] = fit(q)
                x_copy(g, i).start()

                @pl.when(j == 0)
                def _():
                    y_start(g, 3)

                return carry

            lax.fori_loop(0, 3, fit_send, 0)

        @pl.when(t == CHUNKS)
        def _():
            send_rest(CHUNKS - 2)

        @pl.when((t >= 3) & (t < CHUNKS + 3))
        def _():
            g = t - 3
            for j, i in ((0, 3), (2, 0), (3, 2), (1, 1)):
                y_wait(g, j)
                y_forward(g, i).start()
            y_wait(g, 4)
            y_wait(g, 5)
            to_partner(g, ym).start()
            to_partner(g, yp).start()

        @pl.when(t == CHUNKS)
        def _():
            send_rest(CHUNKS - 1)

        @pl.when(t >= 4)
        def _():
            y_wait(t - 4, 6)
            to_partner(t - 4, yo).start()

        @pl.when(t == 2)
        def _():
            for cp in ints_copies() + ens_copies_x():
                cp.wait()
            for cp in small_local:
                cp.wait()
            for cp in ens_copies_y():
                cp.start()

        @pl.when(t == 6)
        def _():
            for cp in ens_copies_y():
                cp.wait()
            to_smem = (
                pltpu.make_async_copy(wanted_v, wanted_s, i_sem.at[2, 3]),
                pltpu.make_async_copy(slots_v, slots_s, i_sem.at[3, 3]),
                pltpu.make_async_copy(ens_v, ens_s, e_sem.at[1, 6]),
            )
            for cp in to_smem:
                cp.start()
            for cp in to_smem:
                cp.wait()

        return carry

    lax.fori_loop(0, CHUNKS + 4, step, 0)

    def sent(ref, sem):
        remote(ref, ref, sem, pr, me_partner).wait_send()

    remote(b_v, b_v, send_sem.at[3], pr, me_partner).wait_recv()
    sent(b_v.at[pl.ds(0, 7)], send_sem.at[0])
    sent(f_v.at[pl.ds(0, 6)], send_sem.at[1])
    sent(b_v.at[pl.ds(0, 6)], send_sem.at[2])
    sent(b_v, send_sem.at[3])
    a_partner.wait_send()

    def orbital(xo, position):
        k = slots_s[xo, 0, position]
        s = k >> 3
        t = wanted_s[xo, k & 7, s]
        return ((t >> 3) << 7) + ((s & 3) << 5) + ((t & 7) << 2) + (s >> 2)

    def pairs(half, first):
        def some(j, carry):
            done = []
            for slot in range(8):
                second = 2 * j + slot // 4
                xo, zz = (first, second) if half == 0 else (second, first)
                n = (2 * zz + c) * 8 + half * 4 + slot % 4
                left = cols[orbital(xo, 2 * n)]
                right = cols[orbital(xo, 2 * n + 1)]
                e = lax.dot_general(left, right, (((1,), (1,)), ((), ())), preferred_element_type=F32)
                done.append((e * SCALE).astype(BF16))
            for slot in range(8):
                part[half, first, j * 8 + slot] = done[slot]
            return carry

        lax.fori_loop(0, 2, some, 0)

    def ring(half, d):
        if half == 0:
            at = (x + d) % 4
            return at, dev(z, c, at, y)
        at = (z + d) % 4
        return at, dev(at, c, x, y)

    def far_copy(half, i):
        far, _ = ring(half, 2)
        _, to = ring(half, 3 if i == 0 else 1)
        return remote(part.at[half, far, pl.ds(8 * i, 8)], rs_far.at[half, i], send_sem.at[4], r_sem.at[0, half, i], to)

    def near_copy(half, i, summed_part):
        at, to = ring(half, 3 if i == 0 else 1)
        first = 8 * i if summed_part else 8 - 8 * i
        j = 2 * i + (1 if summed_part else 0)
        rows = pl.ds(first, 8)
        return remote(part.at[half, at, rows], rs_near.at[half, i, rows], send_sem.at[4], r_sem.at[1, half, j], to)

    def combine(half, i):
        at, _ = ring(half, 3 if i == 0 else 1)
        far_copy(half, i).wait_recv()

        def add(k, carry):
            part[half, at, 8 * i + k] = (part[half, at, 8 * i + k].astype(F32) + rs_far[half, i, k].astype(F32)).astype(BF16)
            return carry

        lax.fori_loop(0, 8, add, 0, unroll=2)

    def rs2_copy(half, d):
        there, to = ring(1 - half, d)
        return remote(summed.at[half, pl.ds(there * 4, 4)], rs2.at[half, d - 1], send_sem.at[5], r_sem.at[2, half, 0], to)

    pairs(0, ring(0, 2)[0])
    pairs(1, ring(1, 2)[0])
    for i in (0, 1):
        far_copy(0, i).start()
        far_copy(1, i).start()
    for i, d in ((0, 3), (1, 1)):
        pairs(0, ring(0, d)[0])
        pairs(1, ring(1, d)[0])
        near_copy(0, i, False).start()
        near_copy(1, i, False).start()
    pairs(0, x)
    pairs(1, z)
    for half in (0, 1):
        for i in (0, 1):
            combine(half, i)
            near_copy(half, i, True).start()

    def out_copy(slot):
        return pltpu.make_async_copy(out_v.at[slot], out.at[0, slot], o_sem)

    live = count[0]

    def energy(position):
        k = slots_s[x, 0, position]
        s = k >> 3
        return ens_s[s & 3, s >> 2, 0, wanted_s[x, k & 7, s]]

    for slot in range(8):
        n = f * 8 + slot
        denom = cabs[...] - (energy(2 * n) + energy(2 * n + 1))
        rec_v[slot] = jnp.where(n < live, 1.0 / denom, 0.0)

    for half in (0, 1):
        me_at = x if half == 0 else z
        for i in (0, 1):
            near_copy(half, i, False).wait_recv()
            near_copy(half, i, True).wait_recv()

        def add(i, carry):
            total = part[half, me_at, i].astype(F32)
            for d in (0, 1):
                total = total + rs_near[half, d, i].astype(F32)
            summed[half, i] = total.astype(BF16)
            return carry

        lax.fori_loop(0, 16, add, 0, unroll=2)
        for d in (2, 1, 3):
            rs2_copy(half, d).start()

    for half in (0, 1):
        me_at = z if half == 0 else x
        remote(rs2.at[half], rs2.at[half], send_sem.at[5], r_sem.at[2, half, 0], me_partner).wait_recv()

        for i in range(4):
            total = summed[half, me_at * 4 + i].astype(F32)
            for d in (0, 1, 2):
                total = total + rs2[half, d, i].astype(F32)
            exchange = total.astype(BF16)
            slot = half * 4 + i
            for at in range(0, 1024, 256):
                at = pl.ds(at, 256)
                weighted = jnp.dot(exchange, coupling[:, at], preferred_element_type=F32)
                out_v[slot, :, at] = (weighted * rec_v[slot, :, at]).astype(BF16)
            if slot:
                out_copy(slot - 1).start()
    out_copy(7).start()

    sent(b_v.at[pl.ds(0, 3)], send_sem.at[4])
    sent(rs2, send_sem.at[5])
    pltpu.make_async_copy(out_v, out.at[0], o_sem).wait()


def on_device(fac, tri, send_map, pair_slots, pair_count, orbital_energy, cabs_energy, coupling):
    dma = pltpu.SemaphoreType.DMA
    ens = jnp.broadcast_to(orbital_energy.astype(F32)[None, :], (8, 16))
    hbm = pl.BlockSpec(memory_space=pl.ANY)
    vmem = pl.BlockSpec(memory_space=pltpu.VMEM)
    return pl.pallas_call(
        fused_kernel,
        out_shape=jax.ShapeDtypeStruct((1, 8, LANES, 1024), BF16),
        in_specs=[hbm, hbm, hbm, hbm, hbm, vmem, vmem, pl.BlockSpec(memory_space=pltpu.SMEM)],
        out_specs=hbm,
        scratch_shapes=[
            pltpu.VMEM((2 * PANEL, 4096), BF16),
            pltpu.VMEM((CHUNKS, 4096, LANES), BF16),
            pltpu.VMEM((CHUNKS, 4, LANES, QROWS), BF16),
            pltpu.VMEM((256, LANES, QROWS), BF16),
            pltpu.VMEM((2, 4, 16, LANES, LANES), BF16),
            pltpu.VMEM((2, 2, 8, LANES, LANES), BF16),
            pltpu.VMEM((2, 2, 16, LANES, LANES), BF16),
            pltpu.VMEM((2, 16, LANES, LANES), BF16),
            pltpu.VMEM((2, 3, 4, LANES, LANES), BF16),
            pltpu.VMEM((4, 8, 16), jnp.int32),
            pltpu.VMEM((4, 1, LANES), jnp.int32),
            pltpu.VMEM((4, 4, 8, 16), F32),
            pltpu.SMEM((4, 8, 16), jnp.int32),
            pltpu.SMEM((4, 1, LANES), jnp.int32),
            pltpu.SMEM((4, 4, 8, 16), F32),
            pltpu.VMEM((8, 1, 1024), F32),
            pltpu.VMEM((8, LANES, 1024), BF16),
            dma((6,)),
            dma((3,)),
            dma((CHUNKS, 3)),
            dma((CHUNKS, 3)),
            dma((CHUNKS, 7)),
            dma,
            dma((4, 4)),
            dma((2, 7)),
            dma((3, 2, 4)),
            dma,
            dma,
        ],
        compiler_params=pltpu.CompilerParams(
            collective_id=0, has_side_effects=True, vmem_limit_bytes=64 * 1024 * 1024 - 65536
        ),
        name="fit_exchange",
    )(fac, tri, jnp.swapaxes(send_map, 1, 2), pair_slots, ens, cabs_energy.reshape(1, 1024), coupling, pair_count)


def solution(mesh):
    in_specs = (
        P("fit", None),
        P("fit", "pair"),
        P("pair", None, None),
        P("pair", None),
        P("pair"),
        P("pair"),
        P(),
        P(),
    )
    return jax.shard_map(
        on_device, mesh=mesh, in_specs=in_specs, out_specs=P("pair", "fit", None, None), check_vma=False
    )
```

time: 148 us -> 141 us (0.953)
  Pallas kernels: 144 us -> 135 us
  local copies, waits for them, and re-layouts: 2.6 us -> 4.33 us
    pallas_call x2 -> x1, Pallas kernels: 144 us -> 135 us  [on_device(): pl.pallas_call(fused_kernel, out_shape=jax.ShapeDtypeStruct((1, 8, LANES,...]
    unnamed x1, local copies, waits for them, and re-layouts: 1.35 us -> 3.08 us
where the time goes in v3:
time: 141 us; the launch traced here: 140 us
  Pallas kernels  135 us (96%)
  local copies, waits for them, and re-layouts  4.33 us (3%)
    pallas_call x1, Pallas kernels, on_device(): pl.pallas_call(fused_kernel, out_shape=jax.ShapeDtypeStruct((1, 8, LANES,...  135 us
    unnamed x1, local copies, waits for them, and re-layouts  3.08 us

profile of v3, /device:TPU:1, one launch (start us, length us, event | category | flops | bytes accessed | tf_op | source)
XLA Modules:
  0.0 140.4 jit_solution(4536016829596940333)
XLA Ops:
  0.7 1.2 broadcast_in_dim.2.ens
  1.9 135.4 %fit_exchange.1 = bf16[1,8,128,1024]{3,2,1,0:T(8,128)(2,1)} custom-call(bf16[512,4096]{1,0:T(8,128)(2,1)} %fac.1, bf16[512,2048]{1,0:T(8,128)(2,1)} %tri.1, s32[1,8,16]{2,1,0:T(8,128)} %bitcast.2, s32[1,128]{1,0:T(1,128)} %slots.1, f32[8,16]{1,0:T(8,128)} %broadcast_in_dim.2.ens, f32[1,1024]{1,0:T(1,128)} %bitcast.3, bf16[128,1024]{1,0:T(8,128)(2,1)} %coupling.1, ...), custom_call_target="tpu_custom_call" | custom-call | tf_op jit(solution)/shard_map/fit_exchange/pallas_call | solution.py:448
  137.3 3.1 %copy.11 = bf16[1,8,128,1024]{3,2,1,0:T(8,128)(2,1)} copy(bf16[1,8,128,1024]{3,2,1,0:T(8,128)(2,1)} %fit_exchange.1) | data formatting | bytes 4194304

commit v4 on v3

--- a/solution.py
+++ b/solution.py
@@ -13,13 +13,14 @@
 PANEL = 512
 QROWS = 256
 SCALE = 4096.0 ** -0.5
+VMEM_LIMIT = 48 * 1024 * 1024
 
 
 def fused_kernel(
-    fac, tri, wanted, slots, ens, cabs, coupling, count,
+    fac, tri, wanted, slots, ens, cabs_hbm, coupling_hbm, count,
     out,
     a_v, b_v, f_v, cols, part, rs_far, rs_near, summed, rs2,
-    wanted_v, slots_v, ens_v, wanted_s, slots_s, ens_s, rec_v, out_v,
+    wanted_v, slots_v, ens_v, wanted_s, slots_s, ens_s, rec_v, cabs, coupling,
     send_sem, a_sem, zr, xr, yr, pr, i_sem, e_sem, r_sem, l_sem, o_sem,
 ):
     f = lax.axis_index("fit")
@@ -148,6 +149,8 @@
         pltpu.make_async_copy(wanted.at[0], wanted_v.at[x], i_sem.at[0, 3]),
         pltpu.make_async_copy(slots, slots_v.at[x], i_sem.at[1, 3]),
         pltpu.make_async_copy(ens, ens_v.at[y, x], e_sem.at[0, 6]),
+        pltpu.make_async_copy(cabs_hbm, cabs, o_sem.at[0]),
+        pltpu.make_async_copy(coupling_hbm, coupling, o_sem.at[1]),
     )
 
     for g in range(CHUNKS):
@@ -385,9 +388,6 @@
             combine(half, i)
             near_copy(half, i, True).start()
 
-    def out_copy(slot):
-        return pltpu.make_async_copy(out_v.at[slot], out.at[0, slot], o_sem)
-
     live = count[0]
 
     def energy(position):
@@ -430,26 +430,22 @@
             for at in range(0, 1024, 256):
                 at = pl.ds(at, 256)
                 weighted = jnp.dot(exchange, coupling[:, at], preferred_element_type=F32)
-                out_v[slot, :, at] = (weighted * rec_v[slot, :, at]).astype(BF16)
-            if slot:
-                out_copy(slot - 1).start()
-    out_copy(7).start()
+                out[0, slot, :, at] = (weighted * rec_v[slot, :, at]).astype(BF16)
 
     sent(b_v.at[pl.ds(0, 3)], send_sem.at[4])
     sent(rs2, send_sem.at[5])
-    pltpu.make_async_copy(out_v, out.at[0], o_sem).wait()
 
 
 def on_device(fac, tri, send_map, pair_slots, pair_count, orbital_energy, cabs_energy, coupling):
     dma = pltpu.SemaphoreType.DMA
     ens = jnp.broadcast_to(orbital_energy.astype(F32)[None, :], (8, 16))
-    hbm = pl.BlockSpec(memory_space=pl.ANY)
+    hbm = pl.BlockSpec(memory_space=pltpu.HBM)
     vmem = pl.BlockSpec(memory_space=pltpu.VMEM)
     return pl.pallas_call(
         fused_kernel,
         out_shape=jax.ShapeDtypeStruct((1, 8, LANES, 1024), BF16),
-        in_specs=[hbm, hbm, hbm, hbm, hbm, vmem, vmem, pl.BlockSpec(memory_space=pltpu.SMEM)],
-        out_specs=hbm,
+        in_specs=[hbm, hbm, hbm, hbm, hbm, hbm, hbm, pl.BlockSpec(memory_space=pltpu.SMEM)],
+        out_specs=vmem,
         scratch_shapes=[
             pltpu.VMEM((2 * PANEL, 4096), BF16),
             pltpu.VMEM((CHUNKS, 4096, LANES), BF16),
@@ -467,7 +463,8 @@
             pltpu.SMEM((4, 1, LANES), jnp.int32),
             pltpu.SMEM((4, 4, 8, 16), F32),
             pltpu.VMEM((8, 1, 1024), F32),
-            pltpu.VMEM((8, LANES, 1024), BF16),
+            pltpu.VMEM((1, 1024), F32),
+            pltpu.VMEM((LANES, 1024), BF16),
             dma((6,)),
             dma((3,)),
             dma((CHUNKS, 3)),
@@ -478,13 +475,19 @@
             dma((2, 7)),
             dma((3, 2, 4)),
             dma,
-            dma,
+            dma((2,)),
         ],
         compiler_params=pltpu.CompilerParams(
-            collective_id=0, has_side_effects=True, vmem_limit_bytes=64 * 1024 * 1024 - 65536
+            collective_id=0, has_side_effects=True, vmem_limit_bytes=VMEM_LIMIT
         ),
         name="fit_exchange",
-    )(fac, tri, jnp.swapaxes(send_map, 1, 2), pair_slots, ens, cabs_energy.reshape(1, 1024), coupling, pair_count)
+    )(
+        *(
+            pltpu.with_memory_space_constraint(a, pltpu.HBM)
+            for a in (fac, tri, jnp.swapaxes(send_map, 1, 2), pair_slots, ens, cabs_energy.reshape(1, 1024), coupling)
+        ),
+        pair_count,
+    )
 
 
 def solution(mesh):

time: 141 us -> 137 us (0.972)
  local copies, waits for them, and re-layouts: 4.33 us -> 2.57 us
    pallas_call x1, Pallas kernels: 135 us -> 134 us  [on_device(): pl.pallas_call(fused_kernel, out_shape=jax.ShapeDtypeStruct((1, 8, LANES,...]
    unnamed x1, local copies, waits for them, and re-layouts: 3.08 us -> 1.32 us
where the time goes in v4:
time: 137 us
  Pallas kernels  134 us (98%)
  local copies, waits for them, and re-layouts  2.57 us (2%)
    pallas_call x1, Pallas kernels, on_device(): pl.pallas_call(fused_kernel, out_shape=jax.ShapeDtypeStruct((1, 8, LANES,...  134 us

profile of v4, /device:TPU:1, one launch (start us, length us, event | category | flops | bytes accessed | tf_op | source)
XLA Modules:
  0.0 136.9 jit_solution(5300000656731970773)
XLA Ops:
  0.7 1.2 broadcast_in_dim.2.ens
  1.9 133.6 %fit_exchange.1 = bf16[1,8,128,1024]{3,2,1,0:T(8,128)(2,1)S(1)} custom-call(bf16[512,4096]{1,0:T(8,128)(2,1)} %fac.1, bf16[512,2048]{1,0:T(8,128)(2,1)} %tri.1, s32[1,8,16]{2,1,0:T(8,128)} %bitcast.2, s32[1,128]{1,0:T(1,128)} %slots.1, f32[8,16]{1,0:T(8,128)} %broadcast_in_dim.2.ens, f32[1,1024]{1,0:T(1,128)} %bitcast.3, bf16[128,1024]{1,0:T(8,128)(2,1)} %coupling_hbm.1, ...), custom_call_target="tpu_custom_call" | custom-call | tf_op jit(solution)/shard_map/fit_exchange/pallas_call | solution.py:444
  135.5 1.3 copy.11

commit v5 on v4

--- a/solution.py
+++ b/solution.py
@@ -321,7 +321,7 @@
         t = wanted_s[xo, k & 7, s]
         return ((t >> 3) << 7) + ((s & 3) << 5) + ((t & 7) << 2) + (s >> 2)
 
-    def pairs(half, first):
+    def pairs(half, first, steps=(0, 2)):
         def some(j, carry):
             done = []
             for slot in range(8):
@@ -336,7 +336,7 @@
                 part[half, first, j * 8 + slot] = done[slot]
             return carry
 
-        lax.fori_loop(0, 2, some, 0)
+        lax.fori_loop(*steps, some, 0)
 
     def ring(half, d):
         if half == 0:
@@ -371,11 +371,14 @@
         there, to = ring(1 - half, d)
         return remote(summed.at[half, pl.ds(there * 4, 4)], rs2.at[half, d - 1], send_sem.at[5], r_sem.at[2, half, 0], to)
 
-    pairs(0, ring(0, 2)[0])
-    pairs(1, ring(1, 2)[0])
+    last = None
     for i in (0, 1):
-        far_copy(0, i).start()
-        far_copy(1, i).start()
+        for half in (0, 1):
+            pairs(half, ring(half, 2)[0], (i, i + 1))
+            if last is not None:
+                last.start()
+            last = far_copy(half, i)
+    last.start()
     for i, d in ((0, 3), (1, 1)):
         pairs(0, ring(0, d)[0])
         pairs(1, ring(1, d)[0])

time: 137 us -> 137 us (level)
  no operation moved by 1% of the time
where the time goes in v5:
time: 137 us
  Pallas kernels  133 us (97%)
  local copies, waits for them, and re-layouts  2.57 us (2%)
    pallas_call x1, Pallas kernels, on_device(): pl.pallas_call(fused_kernel, out_shape=jax.ShapeDtypeStruct((1, 8, LANES,...  133 us

profile of v5, /device:TPU:1, one launch (start us, length us, event | category | flops | bytes accessed | tf_op | source)
XLA Modules:
  0.0 136.6 jit_solution(1446333552024406766)
XLA Ops:
  0.7 1.2 broadcast_in_dim.2.ens
  1.9 133.4 %fit_exchange.1 = bf16[1,8,128,1024]{3,2,1,0:T(8,128)(2,1)S(1)} custom-call(bf16[512,4096]{1,0:T(8,128)(2,1)} %fac.1, bf16[512,2048]{1,0:T(8,128)(2,1)} %tri.1, s32[1,8,16]{2,1,0:T(8,128)} %bitcast.2, s32[1,128]{1,0:T(1,128)} %slots.1, f32[8,16]{1,0:T(8,128)} %broadcast_in_dim.2.ens, f32[1,1024]{1,0:T(1,128)} %bitcast.3, bf16[128,1024]{1,0:T(8,128)(2,1)} %coupling_hbm.1, ...), custom_call_target="tpu_custom_call" | custom-call | tf_op jit(solution)/shard_map/fit_exchange/pallas_call | solution.py:447
  135.3 1.3 copy.11

commit v6 on v5

--- a/solution.py
+++ b/solution.py
@@ -17,7 +17,7 @@
 
 
 def fused_kernel(
-    fac, tri, wanted, slots, ens, cabs_hbm, coupling_hbm, count,
+    fac, tri, wanted, slots, cabs_hbm, coupling_hbm, own_energy, count,
     out,
     a_v, b_v, f_v, cols, part, rs_far, rs_near, summed, rs2,
     wanted_v, slots_v, ens_v, wanted_s, slots_s, ens_s, rec_v, cabs, coupling,
@@ -132,7 +132,7 @@
 
     def ens_copies_x():
         return [
-            remote(ens, ens_v.at[y, x], e_sem.at[0, i], e_sem.at[1, i], dev(z, c, (x + d) % 4, y))
+            remote(ens_v.at[y, x], ens_v.at[y, x], e_sem.at[0, i], e_sem.at[1, i], dev(z, c, (x + d) % 4, y))
             for i, d in enumerate((1, 2, 3))
         ]
 
@@ -148,7 +148,6 @@
     small_local = (
         pltpu.make_async_copy(wanted.at[0], wanted_v.at[x], i_sem.at[0, 3]),
         pltpu.make_async_copy(slots, slots_v.at[x], i_sem.at[1, 3]),
-        pltpu.make_async_copy(ens, ens_v.at[y, x], e_sem.at[0, 6]),
         pltpu.make_async_copy(cabs_hbm, cabs, o_sem.at[0]),
         pltpu.make_async_copy(coupling_hbm, coupling, o_sem.at[1]),
     )
@@ -158,6 +157,11 @@
     a_local.start()
     for cp in small_local:
         cp.start()
+    lane = lax.broadcasted_iota(jnp.int32, (8, 16), 1)
+    tile = jnp.zeros((8, 16), F32)
+    for k in range(16):
+        tile = jnp.where(lane == k, own_energy[k].astype(F32), tile)
+    ens_v[y, x] = tile
 
     pl.semaphore_wait(barrier, len(greeted))
 
@@ -441,13 +445,13 @@
 
 def on_device(fac, tri, send_map, pair_slots, pair_count, orbital_energy, cabs_energy, coupling):
     dma = pltpu.SemaphoreType.DMA
-    ens = jnp.broadcast_to(orbital_energy.astype(F32)[None, :], (8, 16))
     hbm = pl.BlockSpec(memory_space=pltpu.HBM)
     vmem = pl.BlockSpec(memory_space=pltpu.VMEM)
+    smem = pl.BlockSpec(memory_space=pltpu.SMEM)
     return pl.pallas_call(
         fused_kernel,
         out_shape=jax.ShapeDtypeStruct((1, 8, LANES, 1024), BF16),
-        in_specs=[hbm, hbm, hbm, hbm, hbm, hbm, hbm, pl.BlockSpec(memory_space=pltpu.SMEM)],
+        in_specs=[hbm, hbm, hbm, hbm, hbm, hbm, smem, smem],
         out_specs=vmem,
         scratch_shapes=[
             pltpu.VMEM((2 * PANEL, 4096), BF16),
@@ -487,8 +491,9 @@
     )(
         *(
             pltpu.with_memory_space_constraint(a, pltpu.HBM)
-            for a in (fac, tri, jnp.swapaxes(send_map, 1, 2), pair_slots, ens, cabs_energy.reshape(1, 1024), coupling)
+            for a in (fac, tri, jnp.swapaxes(send_map, 1, 2), pair_slots, cabs_energy.reshape(1, 1024), coupling)
         ),
+        pltpu.with_memory_space_constraint(orbital_energy, pltpu.HBM),
         pair_count,
     )
 

time: 137 us -> 136 us (level)
  no operation moved by 1% of the time
where the time goes in v6:
time: 136 us
  Pallas kernels  134 us (99%)
    pallas_call x1, Pallas kernels, on_device(): pl.pallas_call(fused_kernel, out_shape=jax.ShapeDtypeStruct((1, 8, LANES,...  134 us

profile of v6, /device:TPU:1, one launch (start us, length us, event | category | flops | bytes accessed | tf_op | source)
XLA Modules:
  0.0 136.0 jit_solution(5326330327667541316)
XLA Ops:
  0.7 134.0 %fit_exchange.1 = bf16[1,8,128,1024]{3,2,1,0:T(8,128)(2,1)S(1)} custom-call(bf16[512,4096]{1,0:T(8,128)(2,1)} %fac.1, bf16[512,2048]{1,0:T(8,128)(2,1)} %tri.1, s32[1,8,16]{2,1,0:T(8,128)} %bitcast.2, s32[1,128]{1,0:T(1,128)} %slots.1, f32[1,1024]{1,0:T(1,128)} %bitcast.3, bf16[128,1024]{1,0:T(8,128)(2,1)} %coupling_hbm.1, bf16[16]{0:T(256)(128)(2,1)} %own_energy.1, ...), custom_call_target="tpu_custom_call" | custom-call | tf_op jit(solution)/shard_map/fit_exchange/pallas_call | solution.py:451
  134.7 1.3 copy.11
